TPU v7x, 256 devices: a 8x8x2 block of a 8x8x16 slice. The times are simulated.
256 devices in a mesh: replica: 2 (over z), expert: 64 (over y, x), sub: 2 (over core).
Axes of the slice: x: 8, y: 8, z: 2, core: 2. Of those that a mesh axis runs over, the one named last changes fastest.
The devices are a block of a 8x8x16 slice.
Arguments:
- tokens: bfloat16 [2048, 7168], P(('replica', 'expert', 'sub')), parts along dimension 0, may hold values from -6 to 6
- expert_ids: int32 [2048, 8], P(('replica', 'expert', 'sub')), parts along dimension 0, may hold values from 0 to 31, all different within a row; in each aligned block of 8 rows (0 to 7, 8 to 15, ...) at most 3 rows name the same one
- route_levels: int32 [2048, 8], P(('replica', 'expert', 'sub')), parts along dimension 0, may hold values from 1 to 255
- gate_proj: bfloat16 [64, 7168, 512], P('expert', None, 'sub'), may hold values from -0.0625 to 0.0625
- up_proj: bfloat16 [64, 7168, 512], P('expert', None, 'sub'), may hold values from -0.0625 to 0.0625
- down_proj: bfloat16 [64, 512, 7168], P('expert', 'sub'), may hold values from -0.1875 to 0.1875
Outputs:
- moe_out: bfloat16 [2048, 7168], P(('replica', 'expert', 'sub')), parts along dimension 0
There are 2 independent parts, one for each index of `replica`. A program takes and returns all parts, laid end to end along the dimension named above; an argument that names none is the same for every part. Nothing has to cross between parts.
Inputs may be any that keep to these rules, and one draw needn't show every extreme that they name: `expert_ids`: each row names 8 different experts; among the 8 rows of one device no expert is named more than 3 times, and in some devices' rows one is named exactly 3 times.
All inputs are finite; a program needn't handle non-finite values.
Results may differ from a plain program's by a relative error of at most 0.013.
Values may be sent and summed in bfloat16 or wider, within the bound.
A program may use at most 448 MiB of HBM per device.

v0:
```python
import jax
import jax.numpy as jnp
from jax import lax
from jax.sharding import PartitionSpec as P


def cut_along(x, dim, length):
    before, after = (x.shape[:dim], x.shape[dim + 1 :])
    return jnp.moveaxis(x.reshape(*before, length, -1, *after), dim, 0)


def summed_on_arrival(x, axis, dim):
    tiles = cut_along(x, dim, lax.axis_size(axis))
    arrived = lax.all_to_all(tiles, axis, split_axis=0, concat_axis=0, tiled=True)
    return arrived.astype(jnp.float32).sum(axis=0)


def partner_2(block, axis, stride):
    count = lax.axis_size(axis)
    route = []
    for low in range(count):
        high = low | 1 << stride
        if high != low and high < count:
            route += [(low, high), (high, low)]
    return lax.ppermute(block, axis, route)


def laid_out(tiles, dim):
    tiles = jnp.moveaxis(tiles, 0, dim)
    lengths = tiles.shape
    return tiles.reshape(*lengths[:dim], lengths[dim] * lengths[dim + 1], *lengths[dim + 2 :])


def sent_to_all(x, axis):
    length = lax.axis_size(axis)
    return lax.all_to_all(jnp.broadcast_to(x[None], (length, *x.shape)), axis, 0, 0, tiled=True)


def collect(x, axis, dim):
    return laid_out(sent_to_all(x, axis), dim)


def local(tokens, expert_ids, route_levels, gate_proj, up_proj, down_proj):
    rows_here, width = tokens.shape
    picks = expert_ids.shape[1]
    experts = lax.axis_size("expert") * lax.axis_size("sub") // 4
    capacity = rows_here * picks * 3 // (experts * 2)
    pair_count = rows_here * picks
    flat_ids = expert_ids.reshape(pair_count)
    onehot = (flat_ids[:, None] == jnp.arange(experts, dtype=jnp.int32)[None, :]).astype(jnp.int32)
    before = jnp.cumsum(onehot, axis=0, dtype=jnp.int32) - onehot
    slot_of = jnp.sum(before * onehot, axis=1)
    position = flat_ids * capacity + slot_of
    placed = (position[:, None] == jnp.arange(experts * capacity, dtype=jnp.int32)[None, :]).astype(
        jnp.float32
    )
    shares = route_levels.astype(jnp.float32)
    shares = shares / jnp.sum(shares, axis=1, keepdims=True)
    owner_rows = (
        jnp.arange(pair_count, dtype=jnp.int32)[None, :] // picks
        == jnp.arange(rows_here, dtype=jnp.int32)[:, None]
    ).astype(jnp.float32)
    sender = jnp.dot(owner_rows, placed, precision=lax.Precision.HIGHEST)
    weighting = jnp.dot(
        owner_rows * shares.reshape(1, pair_count), placed, precision=lax.Precision.HIGHEST
    )
    outgoing = jnp.dot(sender.T.astype(jnp.bfloat16), tokens, preferred_element_type=jnp.float32)
    outgoing = outgoing.astype(jnp.bfloat16).reshape(experts, 1, capacity, width)
    gate_local = gate_proj[0]
    up_local = up_proj[0]
    down_local = down_proj[0]
    parity = lax.axis_index("expert") % 2
    half_cols = width // 2
    buffer = outgoing.reshape(experts, capacity, 2, half_cols).transpose(0, 2, 1, 3)
    buffer = buffer.reshape(2 * experts, capacity, half_cols)
    arrived = lax.all_to_all(buffer, "expert", split_axis=0, concat_axis=0, tiled=True)
    partner = partner_2(arrived, "expert", 0)
    lower = jnp.where(parity == 0, arrived, partner)
    upper = jnp.where(parity == 0, partner, arrived)
    whole_rows = jnp.concatenate([lower, upper], axis=2)
    both_cores = collect(whole_rows[:, None], "sub", 1)
    leading = both_cores.shape[:-1]
    flat_rows = both_cores.reshape(-1, width)
    gate_vals = jnp.dot(flat_rows, gate_local, preferred_element_type=jnp.float32)
    up_vals = jnp.dot(flat_rows, up_local, preferred_element_type=jnp.float32)
    hidden = (jax.nn.silu(gate_vals) * up_vals).astype(jnp.bfloat16)
    terms = jnp.dot(hidden, down_local, preferred_element_type=jnp.float32).astype(jnp.bfloat16)
    send_terms = terms.reshape(leading + (width,))
    groups, _, items, _ = send_terms.shape
    kept = lax.optimization_barrier(send_terms.reshape(2 * groups, items, width))
    halves = summed_on_arrival(kept.astype(jnp.float32).astype(jnp.bfloat16), "sub", 2)
    fourth = width // 4
    mine = lax.dynamic_slice_in_dim(halves, parity * fourth, fourth, 2)
    other = lax.dynamic_slice_in_dim(halves, (1 - parity) * fourth, fourth, 2)
    total = mine + partner_2(other.astype(jnp.bfloat16), "expert", 0).astype(other.dtype)
    back = lax.all_to_all(
        total.astype(jnp.bfloat16), ("expert", "sub"), split_axis=0, concat_axis=0, tiled=True
    )
    arranged = back.reshape(groups // 2, 2, 2, items, fourth).transpose(0, 3, 2, 1, 4)
    returned = arranged.reshape(groups // 2, items, width)
    results = jnp.sum(returned.reshape(experts, -1, capacity, width), axis=1, dtype=jnp.float32)
    rounded = lax.optimization_barrier(
        results.reshape(experts * capacity, width).astype(jnp.bfloat16)
    )
    mixed = jnp.dot(
        weighting,
        rounded.astype(jnp.float32),
        precision=lax.Precision.HIGHEST,
        preferred_element_type=jnp.float32,
    )
    return mixed.astype(jnp.bfloat16)


def solution(mesh):
    return jax.shard_map(
        local,
        mesh=mesh,
        in_specs=(
            P(("replica", "expert", "sub"), None),
            P(("replica", "expert", "sub"), None),
            P(("replica", "expert", "sub"), None),
            P("expert", None, "sub"),
            P("expert", None, "sub"),
            P("expert", "sub", None),
        ),
        out_specs=P(("replica", "expert", "sub"), None),
        check_vma=False,
    )
```

profile of v0, /device:TPU:514, one launch (start us, length us, event | category | flops | bytes accessed | tf_op | source)
XLA Modules:
  0.0 289.2 jit_solution(7033853999286134103)
XLA Ops:
  0.0 0.0 copy-start
  0.0 0.8 reshape.71
  0.8 0.1 fusion.12
  0.9 0.1 reduce_window_sum.11
  1.0 0.2 select_reduce_fusion
  1.2 0.2 convolution_convert_fusion.3
  1.4 0.0 copy-done
  1.4 0.6 convolution_convert_fusion.1
  1.9 1.0 reshape_reshape.12
  3.0 0.7 copy.37
  3.7 66.0 %all_to_all.20 = bf16[64,3,3584]{2,1,0:T(4,128)(2,1)S(1)} all-to-all(bf16[64,3,3584]{2,1,0:T(4,128)(2,1)S(1)} %bitcast.37), channel_id=1, replica_groups=mesh['replica'=2,'expert'=64,'sub'=2] {'expert'}, dimensions={0} | all-to-all | bytes 2752512 | tf_op jit(solution)/shard_map/all_to_all | solution.py:76
  69.7 1.4 copy.26
  71.1 0.7 collective-permute-start
  71.8 26.0 %collective-permute-done = bf16[64,3,3584]{2,0,1:T(8,128)(2,1)S(1)} collective-permute-done((bf16[64,3,3584]{2,0,1:T(8,128)(2,1)}, bf16[64,3,3584]{2,0,1:T(8,128)(2,1)S(1)}, u32[]{:S(2)}, u32[]{:S(2)}) %collective-permute-start) | collective-permute-done | bytes 1376288 | tf_op jit(solution)/shard_map/ppermute | solution.py:25
  97.8 2.9 %broadcast_select_fusion.1 = (bf16[64,3,3584]{2,1,0:T(4,128)(2,1)S(1)}, bf16[64,3,3584]{2,1,0:T(4,128)(2,1)S(1)}) fusion(bf16[64,3,3584]{2,1,0:T(4,128)(2,1)S(1)} %all_to_all.20, pred[]{:T(512)S(6)} %eq.60, bf16[64,3,3584]{2,0,1:T(8,128)(2,1)S(1)} %collective-permute-done), kind=kLoop, calls=%fused_computation.13 | loop fusion | flops 1376256 | bytes 5505025 | tf_op jit(solution)/shard_map/jit(_where)/select_n | solution.py:78
  100.7 1.6 pad_maximum_fusion
  102.3 1.1 copy.29
  103.4 0.6 broadcast_in_dim.2
  104.0 9.4 %all_to_all.21 = bf16[2,64,1,3,7168]{4,1,3,2,0:T(8,128)(2,1)} all-to-all(bf16[2,64,1,3,7168]{4,1,3,2,0:T(8,128)(2,1)S(1)} %broadcast_in_dim.2), channel_id=1, replica_groups=mesh['replica'=2,'expert'=64,'sub'=2] {'sub'}, dimensions={0} | all-to-all | bytes 11010048 | tf_op jit(solution)/shard_map/all_to_all | solution.py:36
  113.4 10.2 %copy.30 = bf16[64,2,1,3,7168]{4,3,1,0,2:T(4,128)(2,1)} copy(bf16[64,2,1,3,7168]{4,0,3,2,1:T(8,128)(2,1)} %bitcast.34) | data formatting | bytes 11010048 | tf_op jit(solution)/shard_map/transpose | solution.py:29
  123.6 13.0 %reshape_reshape.13 = bf16[384,7168]{1,0:T(8,128)(2,1)} reshape(bf16[64,2,1,3,7168]{4,3,1,0,2:T(4,128)(2,1)} %copy.30) | data formatting | bytes 11010048 | tf_op jit(solution)/shard_map/reshape;reshape | solution.py:83
  136.6 5.4 %fusion.3 = f32[384,256]{1,0:T(8,128)S(1)} fusion(bf16[384,7168]{1,0:T(8,128)(2,1)} %reshape_reshape.13, bf16[1,7168,256]{2,1,0:T(8,128)(2,1)} %param.9), kind=kOutput, calls=%fused_computation.8 | convolution fusion | flops 1409286144 | bytes 9568256 | tf_op jit(solution)/shard_map/dot_general | solution.py:84
  142.0 0.9 copy-done.6
  143.0 1.6 fusion.8
  144.5 0.4 copy-done.4
  145.0 4.0 %convolution_convert_fusion = bf16[384,7168]{1,0:T(8,128)(2,1)} fusion(bf16[384,256]{1,0:T(8,128)(2,1)S(1)} %fusion.8, bf16[1,256,7168]{2,1,0:T(8,128)(2,1)S(1)} %copy-done.4), kind=kOutput, calls=%fused_computation.1 | convolution fusion | flops 1412038656 | bytes 9371648 | tf_op jit(solution)/shard_map/dot_general | solution.py:87
  149.0 12.3 %reshape_reshape.14 = bf16[128,3,7168]{2,1,0:T(4,128)(2,1)} reshape(bf16[384,7168]{1,0:T(8,128)(2,1)} %convolution_convert_fusion) | data formatting | bytes 11010048 | tf_op jit(solution)/shard_map/reshape;reshape | solution.py:90
  161.3 12.1 %copy.31 = bf16[128,3,7168]{0,2,1:T(8,128)(2,1)} copy(bf16[128,3,7168]{2,1,0:T(4,128)(2,1)} %reshape_reshape.14) | data formatting | bytes 11010048 | tf_op jit(solution)/shard_map/optimization_barrier | solution.py:90
  173.4 2.9 %copy.32 = bf16[2,128,3,3584]{1,3,2,0:T(8,128)(2,1)S(1)} copy(bf16[2,128,3,3584]{1,3,0,2:T(8,128)(2,1)} %bitcast.35) | data formatting | bytes 11010048 | tf_op jit(solution)/shard_map/transpose | solution.py:9
  176.3 8.2 %all_to_all.22 = bf16[2,128,3,3584]{1,3,2,0:T(8,128)(2,1)S(1)} all-to-all(bf16[2,128,3,3584]{1,3,2,0:T(8,128)(2,1)S(1)} %copy.32), channel_id=1, replica_groups=mesh['replica'=2,'expert'=64,'sub'=2] {'sub'}, dimensions={0} | all-to-all | bytes 11010048 | tf_op jit(solution)/shard_map/all_to_all | solution.py:14
  184.5 1.0 convert_reduce_fusion
  185.4 2.4 copy-done.2
  187.8 0.2 dynamic-slice_convert_fusion
  188.0 0.6 collective-permute-start.1
  188.6 31.9 %collective-permute-done.1 = bf16[128,3,1792]{0,2,1:T(8,128)(2,1)S(1)} collective-permute-done((bf16[128,3,1792]{0,2,1:T(8,128)(2,1)S(1)}, bf16[128,3,1792]{0,2,1:T(8,128)(2,1)S(1)}, u32[]{:S(2)}, u32[]{:S(2)}) %collective-permute-start.1) | collective-permute-done | bytes 1376288 | tf_op jit(solution)/shard_map/ppermute | solution.py:25
  220.6 2.0 add_convert_fusion
  222.6 0.0 copy-start.5
  222.6 3.3 %copy.34 = bf16[128,3,1792]{2,1,0:T(4,128)(2,1)} copy(bf16[128,3,1792]{0,2,1:T(8,128)(2,1)S(1)} %add_convert_fusion) | data formatting | bytes 2752512 | tf_op jit(solution)/shard_map/convert_element_type | solution.py:97
  225.9 12.5 %all-to-all-start.3 = ((bf16[128,3,1792]{2,1,0:T(4,128)(2,1)}), bf16[128,3,1792]{2,1,0:T(4,128)(2,1)S(1)}, u32[]{:S(2)}, u32[]{:S(2)}) async-start(bf16[128,3,1792]{2,1,0:T(4,128)(2,1)} %copy.34), calls=%async_computation.3 | async-start | bytes 3670016 | tf_op jit(solution)/shard_map/all_to_all | solution.py:96
  238.4 0.1 convert_reduce_fusion.1
  238.5 0.1 convert_divide_fusion
  238.6 0.1 mul.34
  238.7 0.2 fusion.11
  238.9 46.8 %all-to-all-done.3 = bf16[128,3,1792]{2,1,0:T(4,128)(2,1)S(1)} async-done(((bf16[128,3,1792]{2,1,0:T(4,128)(2,1)}), bf16[128,3,1792]{2,1,0:T(4,128)(2,1)S(1)}, u32[]{:S(2)}, u32[]{:S(2)}) %all-to-all-start.3) | async-done | bytes 1376288 | tf_op jit(solution)/shard_map/all_to_all | solution.py:96
  285.6 1.2 copy.47
  286.8 1.1 reshape_reshape.15
  287.9 1.3 convolution_convert_fusion.2
  289.2 0.0 copy-done.1
  (8 shorter events, 0.0 us)
Async XLA Ops:
  0.0 1.4 copy-start
  71.1 26.7 %collective-permute-start = (bf16[64,3,3584]{2,0,1:T(8,128)(2,1)}, bf16[64,3,3584]{2,0,1:T(8,128)(2,1)S(1)}, u32[]{:S(2)}, u32[]{:S(2)}) collective-permute-start(bf16[64,3,3584]{2,0,1:T(8,128)(2,1)} %copy.26), channel_id=1, source_target_pairs={{0,2},{2,0},{4,6},{6,4},{8,10},{10,8},{12,14},{14,12},{16,18},{18,... | collective-permute-start | bytes 4128776 | tf_op jit(solution)/shard_map/ppermute | solution.py:25
  136.6 5.4 %copy-start.3 = (bf16[384,7168]{1,0:T(8,128)(2,1)S(1)}, bf16[384,7168]{1,0:T(8,128)(2,1)}, u32[]{:S(2)}) copy-start(bf16[384,7168]{1,0:T(8,128)(2,1)} %reshape_reshape.13) | copy-start | bytes 16515076
  136.6 6.3 %copy-start.6 = (bf16[1,7168,256]{2,1,0:T(8,128)(2,1)S(1)}, bf16[1,7168,256]{2,1,0:T(8,128)(2,1)}, u32[]{:S(2)}) copy-start(bf16[1,7168,256]{2,1,0:T(8,128)(2,1)} %param.10) | copy-start | bytes 11010052
  143.0 2.0 copy-start.4
  185.4 2.4 copy-start.2
  188.0 32.6 %collective-permute-start.1 = (bf16[128,3,1792]{0,2,1:T(8,128)(2,1)S(1)}, bf16[128,3,1792]{0,2,1:T(8,128)(2,1)S(1)}, u32[]{:S(2)}, u32[]{:S(2)}) collective-permute-start(bf16[128,3,1792]{0,2,1:T(8,128)(2,1)S(1)} %dynamic-slice_convert_fusion), channel_id=1, source_target_pairs={{0,2},{2,0},{4,6},{6,4},{8,10},{10,8},{12,14},{14,12},{16,18},{18,... | collective-permute-start | bytes 4128776 | tf_op jit(solution)/shard_map/ppermute | solution.py:25
  222.6 15.8 %copy-start.5 = (s32[8,8]{1,0:T(8,128)S(1)}, s32[8,8]{1,0:T(8,128)}, u32[]{:S(2)}) copy-start(s32[8,8]{1,0:T(8,128)} %param.8) | copy-start | bytes 772
  225.9 59.7 %all-to-all-start.3 = ((bf16[128,3,1792]{2,1,0:T(4,128)(2,1)}), bf16[128,3,1792]{2,1,0:T(4,128)(2,1)S(1)}, u32[]{:S(2)}, u32[]{:S(2)}) async-start(bf16[128,3,1792]{2,1,0:T(4,128)(2,1)} %copy.34), calls=%async_computation.3 | async-start | bytes 3670016 | tf_op jit(solution)/shard_map/all_to_all | solution.py:96
  285.6 3.6 %copy-start.1 = (bf16[8,7168]{1,0:T(8,128)(2,1)S(1)}, bf16[8,7168]{1,0:T(8,128)(2,1)}, u32[]{:S(2)}) copy-start(bf16[8,7168]{1,0:T(8,128)(2,1)} %param.6) | copy-start | bytes 344068
where the time goes:
time: 295 us; the launch traced here: 289 us
  waiting for transfers between devices  105 us (36%)
  blocking collectives  83.5 us (28%)
  local copies, waits for them, and re-layouts  65.8 us (22%)
  starting transfers between devices  13.8 us (5%)
  matrix products  13.2 us (4%)
  other arithmetic  8.02 us (3%)
    all_to_all x1, blocking collectives, local(): lax.all_to_all(buffer, 'expert', split_axis=0, concat_axis=0, tiled=True)  66 us
    ppermute x2, waiting for transfers between devices, partner_2(): return lax.ppermute(block, axis, route)  57.9 us
    all_to_all x1, waiting for transfers between devices, local(): lax.all_to_all(total.astype(jnp.bfloat16), ('expert', 'sub'), split_axis=...  46.8 us
    another operation x1, local copies, waits for them, and re-layouts, local(): flat_rows = both_cores.reshape(-1, width)  13 us
    all_to_all x1, starting transfers between devices, local(): lax.all_to_all(total.astype(jnp.bfloat16), ('expert', 'sub'), split_axis=...  12.5 us
    another operation x1, local copies, waits for them, and re-layouts, local(): send_terms.reshape(2 * groups, items, width)  12.3 us
    optimization_barrier x1, local copies, waits for them, and re-layouts, local(): lax.optimization_barrier(send_terms.reshape(2 * groups, items, width))  12.1 us
    transpose x1, local copies, waits for them, and re-layouts, laid_out(): tiles = jnp.moveaxis(tiles, 0, dim)  10.2 us
  transfers between devices with their start and end apart: 3, of which 3 were waited for; matrix products, arithmetic and copies ran while one was open for 0% of the time, Pallas kernels for 0%

commit v1 on v0

v1 whole, which is shorter than its diff:
```python
import jax
import jax.numpy as jnp
from jax import lax
from jax.sharding import PartitionSpec as P


def local(tokens, expert_ids, route_levels, gate_proj, up_proj, down_proj):
    rows, width = tokens.shape
    experts = lax.axis_size("expert") // 2
    levels = jnp.sum(
        jnp.where(expert_ids[:, :, None] == jnp.arange(128, dtype=jnp.int32), route_levels[:, :, None], 0),
        axis=1,
    )
    carried = jnp.concatenate([tokens, levels.astype(jnp.bfloat16)], axis=1)
    everyone = lax.all_gather(carried, ("expert", "sub"), axis=0, tiled=True)
    x = everyone[:, :width]
    level = everyone[:, width:].astype(jnp.float32)
    mine = jnp.arange(128, dtype=jnp.int32) == lax.axis_index("expert") // 2
    share = jnp.sum(jnp.where(mine, level, 0.0), axis=1, keepdims=True) / jnp.sum(level, axis=1, keepdims=True)
    gate = jnp.dot(x, gate_proj[0], preferred_element_type=jnp.float32)
    up = jnp.dot(x, up_proj[0], preferred_element_type=jnp.float32)
    hidden = (jax.nn.silu(gate) * up * share).astype(jnp.bfloat16)
    part = jnp.dot(hidden, down_proj[0], preferred_element_type=jnp.float32).astype(jnp.bfloat16)
    return lax.psum_scatter(part, ("expert", "sub"), scatter_dimension=0, tiled=True)


def solution(mesh):
    return jax.shard_map(
        local,
        mesh=mesh,
        in_specs=(
            P(("replica", "expert", "sub"), None),
            P(("replica", "expert", "sub"), None),
            P(("replica", "expert", "sub"), None),
            P("expert", None, "sub"),
            P("expert", None, "sub"),
            P("expert", "sub", None),
        ),
        out_specs=P(("replica", "expert", "sub"), None),
        check_vma=False,
    )
```

time: 295 us -> 367 us (1.24); the launches traced: 289 us -> 367 us
  waiting for transfers between devices: 105 us -> 325 us
  blocking collectives: 83.5 us -> 0 us
  local copies, waits for them, and re-layouts: 65.8 us -> 0.01 us
  starting transfers between devices: 13.8 us -> 0.07 us
  between operations: 0.17 us -> 13.5 us
  matrix products: 13.2 us -> 25.2 us
  other arithmetic: 8.02 us -> 3.55 us
    reduce_scatter x0 -> x1, waiting for transfers between devices: none -> 213 us  [local(): lax.psum_scatter(part, ('expert', 'sub'), scatter_dimension=0, tiled=True)]
    all_gather x0 -> x1, waiting for transfers between devices: none -> 111 us  [local(): everyone = lax.all_gather(carried, ('expert', 'sub'), axis=0, tiled=True)]
    all_to_all x3 -> x0, blocking collectives: 83.5 us -> none  [the longest x1 66 us: local(): lax.all_to_all(buffer, 'expert', split_axis=0, concat_axis=0, tiled=True)]
    ppermute x2 -> x0, waiting for transfers between devices: 57.9 us -> none  [partner_2(): return lax.ppermute(block, axis, route)]
    all_to_all x1 -> x0, waiting for transfers between devices: 46.8 us -> none  [local(): lax.all_to_all(total.astype(jnp.bfloat16), ('expert', 'sub'), split_axis=...]
    another operation x4 -> x0, local copies, waits for them, and re-layouts: 27.4 us -> none  [the longest x1 13 us: local(): flat_rows = both_cores.reshape(-1, width)]
    transpose x3 -> x0, local copies, waits for them, and re-layouts: 14.3 us -> none  [the longest x1 10.2 us: laid_out(): tiles = jnp.moveaxis(tiles, 0, dim)]
    all_to_all x1 -> x0, starting transfers between devices: 12.5 us -> none  [local(): lax.all_to_all(total.astype(jnp.bfloat16), ('expert', 'sub'), split_axis=...]
  transfers between devices with their start and end apart: 3 -> 2, of which waited for: 3 -> 2; matrix products, arithmetic and copies ran while one was open for 0% -> 0% of each run, Pallas kernels for 0% -> 0%
where the time goes in v1:
time: 367 us
  waiting for transfers between devices  325 us (89%)
  matrix products  25.2 us (7%)
  between operations  13.5 us (4%)
    reduce_scatter x1, waiting for transfers between devices, local(): lax.psum_scatter(part, ('expert', 'sub'), scatter_dimension=0, tiled=True)  213 us
    all_gather x1, waiting for transfers between devices, local(): everyone = lax.all_gather(carried, ('expert', 'sub'), axis=0, tiled=True)  111 us
    dot_general x1, matrix products, local(): up = jnp.dot(x, up_proj[0], preferred_element_type=jnp.float32)  9.36 us
    dot_general x1, matrix products, local(): gate = jnp.dot(x, gate_proj[0], preferred_element_type=jnp.float32)  8.45 us
    dot_general x1, matrix products, local(): jnp.dot(hidden, down_proj[0], preferred_element_type=jnp.float32)  7.38 us
  transfers between devices with their start and end apart: 2, of which 2 were waited for; matrix products, arithmetic and copies ran while one was open for 0% of the time, Pallas kernels for 0%

profile of v1, /device:TPU:514, one launch (start us, length us, event | category | flops | bytes accessed | tf_op | source)
XLA Modules:
  0.0 366.8 jit_solution(16336927684279294206)
XLA Ops:
  6.5 0.0 all-gather.2.cloned.1.call-start
  6.6 0.8 select_reduce_fusion
  7.4 1.5 pad_maximum_fusion
  8.9 0.1 all-gather.2.cloned.1.call-update
  9.0 0.1 reduce-scatter.2.cloned.1.call-start
  9.1 111.2 %all-gather.2.cloned.1.call-done = bf16[1024,7296]{1,0:T(8,128)(2,1)} async-done(((bf16[8,7296]{1,0:T(8,128)(2,1)}), bf16[1024,7296]{1,0:T(8,128)(2,1)}) %all-gather.2.cloned.1.call-update) | async-done | bytes 14942224 | tf_op jit(solution)/shard_map/all_gather | solution.py:15
  120.2 1.2 convert_reduce_fusion
  121.4 0.0 copy-start.1
  121.5 8.5 %fusion.2 = f32[1024,256]{1,0:T(8,128)S(1)} fusion(bf16[1024,7296]{1,0:T(8,128)(2,1)} %all-gather.2.cloned.1.call-done, bf16[1,7168,256]{2,1,0:T(8,128)(2,1)} %param.9), kind=kOutput, calls=%fused_computation.3 | convolution fusion | flops 3758096384 | bytes 19398656 | tf_op jit(solution)/shard_map/dot_general | solution.py:20
  129.9 0.0 copy-done.1
  129.9 0.0 copy-start
  129.9 9.4 %fusion.17 = bf16[1024,256]{1,0:T(8,128)(2,1)S(1)} fusion(bf16[1,7168,256]{2,1,0:T(8,128)(2,1)S(1)} %copy-done.1, bf16[1024,7296]{1,0:T(8,128)(2,1)} %all-gather.2.cloned.1.call-done, f32[1024,256]{1,0:T(8,128)S(1)} %fusion.2, f32[1024]{0:T(1024)S(1)} %div.24), kind=kOutput, calls=%fused_computation.10 | convolution fusion | flops 3759931392 | bytes 19927040 | tf_op jit(solution)/shard_map/dot_general | solution.py:21
  139.3 0.0 copy-done
  139.3 7.4 %convolution_convert_fusion = bf16[1024,7168]{1,0:T(8,128)(2,1)} fusion(bf16[1024,256]{1,0:T(8,128)(2,1)S(1)} %fusion.17, bf16[1,256,7168]{2,1,0:T(8,128)(2,1)S(1)} %copy-done), kind=kOutput, calls=%fused_computation | convolution fusion | flops 3765436416 | bytes 18874368 | tf_op jit(solution)/shard_map/dot_general | solution.py:23
  146.7 0.1 reduce-scatter.2.cloned.1.call-update
  146.8 213.2 %reduce-scatter.2.cloned.1.call-done = bf16[8,7168]{1,0:T(8,128)(2,1)} async-done(((bf16[1024,7168]{1,0:T(8,128)(2,1)}), bf16[8,7168]{1,0:T(8,128)(2,1)}) %reduce-scatter.2.cloned.1.call-update) | async-done | bytes 114704 | tf_op jit(solution)/shard_map/reduce_scatter | solution.py:24
  (3 shorter events, 0.0 us)
Async XLA Ops:
  6.5 113.7 %all-gather.2.cloned.1.call-start = ((), (), s32[]{:S(2)}) async-start(), calls=%async_computation.1 | async-start | bytes 15058944 | tf_op jit(solution)/shard_map/all_gather | solution.py:15
  9.0 351.0 %reduce-scatter.2.cloned.1.call-start = ((), (), s32[]{:S(2)}) async-start(), calls=%async_computation.2 | async-start | bytes 14794752 | tf_op jit(solution)/shard_map/reduce_scatter | solution.py:24
  121.4 8.5 %copy-start.1 = (bf16[1,7168,256]{2,1,0:T(8,128)(2,1)S(1)}, bf16[1,7168,256]{2,1,0:T(8,128)(2,1)}, u32[]{:S(2)}) copy-start(bf16[1,7168,256]{2,1,0:T(8,128)(2,1)} %param.10) | copy-start | bytes 11010052
  129.9 9.4 %copy-start = (bf16[1,256,7168]{2,1,0:T(8,128)(2,1)S(1)}, bf16[1,256,7168]{2,1,0:T(8,128)(2,1)}, u32[]{:S(2)}) copy-start(bf16[1,256,7168]{2,1,0:T(8,128)(2,1)} %param.11) | copy-start | bytes 11010052
Sparse Core Ops, SparseCore 0:
  10.0 110.1 all-gather.1
  146.9 213.0 reduce-scatter.1

commit v2 on v1

v2 whole, which is shorter than its diff:
```python
import functools
import math

import jax
import jax.numpy as jnp
from jax import lax
from jax.experimental import pallas as pl
from jax.experimental.pallas import tpu as pltpu
from jax.sharding import PartitionSpec as P

BF16, F32 = jnp.bfloat16, jnp.float32
LANES = 128
ORDER = (0, -1, 1, -2, 2, -3, 3, 4)
FORWARD, BACKWARD = 0, 1
HALF_RANKS = ((7, 6, 5, 4), (3, 2, 1, 0))
BLOCKS = ((0, 9), (9, 25), (25, 49), (49, 64))


def reach(place):
    return min(place % 8, -place % 8)


def slots():
    cells = [(y, x) for y in range(8) for x in range(8)]
    cells.sort(key=lambda c: max(reach(c[0]), reach(c[1])))
    return {cell: i for i, cell in enumerate(cells)}


SLOT = slots()


def slot(y, x):
    return SLOT[(y % 8, x % 8)]


def block_of(index):
    return next(b for b, (lo, hi) in enumerate(BLOCKS) if lo <= index < hi)


def kernel(
    tokens, levels, gate, up, down, out,
    x, w, wd, hs, hr, p, p0, r, s, rs, ss, osend, orecv,
    in_sem, w_sem, pair_send, pair_recv,
    g1_send, g1_recv, g2_send, g2_recv, d_send, d_recv, h_send, h_recv,
    b_send, b_recv, c_send, c_recv, o_send, o_recv,
):
    rows, width = tokens.shape
    half = width // 2
    part = half // 2
    chunk = 2 * rows
    side = math.isqrt(lax.axis_size("expert"))
    me = lax.axis_index("expert")
    core = lax.axis_index("sub")
    my_y, my_x = me // side, me % side
    quarter = hs.shape[1]
    other_at = half + LANES
    mine_from = pl.multiple_of(core * half, LANES)
    theirs_from = pl.multiple_of((1 - core) * half, LANES)
    sibling = {"sub": 1 - core}

    def neighbour(along_x, direction):
        step = 1 if direction == FORWARD else side - 1
        if along_x:
            return {"expert": my_y * side + (my_x + step) % side}
        return {"expert": ((my_y + step) % side) * side + my_x}

    lanes_of = (pl.ds(part, part + LANES), pl.ds(0, part))
    data_of = (pl.ds(part, part), pl.ds(0, part))
    there_of = (pl.ds(other_at + part, part), pl.ds(other_at, part))
    cut = ((pl.ds(part, 8 * LANES), pl.ds(part + 8 * LANES, 7 * LANES)), (pl.ds(0, part // 2), pl.ds(part // 2, part // 2)))

    def rows_of(index, count=1):
        return pl.ds(index * chunk, count * chunk)

    def remote(src, dst, send, recv, device):
        return pltpu.make_async_remote_copy(
            src_ref=src, dst_ref=dst, send_sem=send, recv_sem=recv, device_id=device,
            device_id_type=pl.DeviceIdType.MESH,
        )

    own_rows = pl.ds(pl.multiple_of(core * rows, rows), rows)
    loads = [
        pltpu.make_async_copy(tokens.at[:, pl.ds(mine_from, half)], x.at[own_rows, pl.ds(0, half)], in_sem.at[0]),
        pltpu.make_async_copy(levels, x.at[own_rows, pl.ds(half, LANES)], in_sem.at[1]),
        pltpu.make_async_copy(tokens.at[:, pl.ds(theirs_from, half)], x.at[own_rows, pl.ds(other_at, half)], in_sem.at[2]),
    ]
    weights = []
    for i, m in enumerate((gate, up)):
        for j, start in enumerate((mine_from, theirs_from)):
            weights.append(
                pltpu.make_async_copy(
                    m.at[0, pl.ds(start, half), :],
                    w.at[pl.ds(j * half, half), pl.ds(i * quarter, quarter)],
                    w_sem.at[2 * i + j],
                )
            )
    weights.append(pltpu.make_async_copy(down.at[0, :, pl.ds(mine_from, half)], wd.at[pl.ds(0, quarter), :], w_sem.at[4]))
    for c in loads + weights:
        c.start()

    barrier = pltpu.get_barrier_semaphore()
    for device in (
        sibling,
        neighbour(True, FORWARD),
        neighbour(True, BACKWARD),
        neighbour(False, FORWARD),
        neighbour(False, BACKWARD),
    ):
        pl.semaphore_signal(barrier, inc=1, device_id=device, device_id_type=pl.DeviceIdType.MESH)
    pl.semaphore_wait(barrier, 5)

    swaps = [
        remote(tokens.at[:, pl.ds(theirs_from, half)], x.at[own_rows, pl.ds(0, half)], pair_send.at[0], pair_recv.at[0], sibling),
        remote(levels, x.at[own_rows, pl.ds(half, LANES)], pair_send.at[1], pair_recv.at[1], sibling),
        remote(tokens.at[:, pl.ds(mine_from, half)], x.at[own_rows, pl.ds(other_at, half)], pair_send.at[2], pair_recv.at[2], sibling),
        remote(down.at[0, :, pl.ds(theirs_from, half)], wd.at[pl.ds(quarter, quarter), :], pair_send.at[3], pair_recv.at[3], sibling),
    ]
    for c in swaps:
        c.start()

    def cell(which, along, across):
        return slot(across, along) if which == 0 else slot(along, across)

    def line_copy(which, direction, k):
        sign = -1 if direction == FORWARD else 1
        lanes = lanes_of[which] if k < 4 else cut[which][direction]
        i = 4 * (2 * which + direction) + k - 1
        return remote(
            x.at[rows_of(cell(which, sign * (k - 1), 0)), lanes],
            x.at[rows_of(cell(which, sign * k, 0)), lanes],
            g1_send.at[i], g1_recv.at[i], neighbour(which == 0, direction),
        )

    def plane_copy(which, direction, k, rank):
        sign = -1 if direction == FORWARD else 1
        st = 2 * which + direction
        i = 28 * st + (8 * (k - 1) + rank if k < 4 else 24 + HALF_RANKS[direction].index(rank))
        return remote(
            x.at[rows_of(cell(which, ORDER[rank], sign * (k - 1))), lanes_of[which]],
            x.at[rows_of(cell(which, ORDER[rank], sign * k)), lanes_of[which]],
            g2_send.at[st], g2_recv.at[i], neighbour(which == 1, direction),
        )

    def hand_over(which, index):
        b = block_of(index)
        remote(
            x.at[rows_of(index), data_of[which]], x.at[rows_of(index), there_of[which]],
            d_send.at[b], d_recv.at[b], sibling,
        ).start()

    streams = [(which, direction) for which in (0, 1) for direction in (FORWARD, BACKWARD)]

    def line_arrives(k):
        for which, direction in streams:
            sign = -1 if direction == FORWARD else 1
            line_copy(which, direction, k).wait_recv()
            if k < 4:
                line_copy(which, direction, k + 1).start()
                rank = ORDER.index(sign * k)
                for d in (FORWARD, BACKWARD):
                    plane_copy(which, d, 1, rank).start()
                hand_over(which, cell(which, sign * k, 0))
        if k == 4:
            for which in (0, 1):
                for d in (FORWARD, BACKWARD):
                    plane_copy(which, d, 1, 7).start()
                hand_over(which, cell(which, 4, 0))

    def plane_arrives(k, rank):
        for which, direction in streams:
            sign = -1 if direction == FORWARD else 1
            if k == 4 and rank not in HALF_RANKS[direction]:
                continue
            plane_copy(which, direction, k, rank).wait_recv()
            if k < 3 or (k == 3 and rank in HALF_RANKS[direction]):
                plane_copy(which, direction, k + 1, rank).start()
            hand_over(which, cell(which, ORDER[rank], sign * k))

    def hidden_copy(b):
        lo, hi = BLOCKS[b]
        span = rows_of(lo, hi - lo)
        return remote(hs.at[span, :], hr.at[span, :], h_send.at[b], h_recv.at[b], sibling)

    def handed(b):
        lo, hi = BLOCKS[b]
        lo = max(lo, 1)
        span = rows_of(lo, hi - lo)
        return remote(x.at[span, pl.ds(0, half)], x.at[span, pl.ds(other_at, half)], d_send.at[b], d_recv.at[b], sibling)

    def compute(b):
        lo, hi = BLOCKS[b]
        handed(b).wait_recv()
        if b == 0:
            for c in weights[:4]:
                c.wait()
        span = rows_of(lo, hi - lo)
        pre = jnp.dot(x[span, pl.ds(0, half)], w[pl.ds(0, half), :], preferred_element_type=F32)
        pre += jnp.dot(x[span, pl.ds(other_at, half)], w[pl.ds(half, half), :], preferred_element_type=F32)
        level = x[span, pl.ds(half, LANES)].astype(F32)
        lane = lax.broadcasted_iota(jnp.int32, level.shape, 1)
        share = jnp.sum(jnp.where(lane == me // 2, level, 0.0), axis=1, keepdims=True)
        share = share / jnp.sum(level, axis=1, keepdims=True)
        g, u = pre[:, :quarter], pre[:, quarter:]
        hs[span, :] = (g / (1.0 + jnp.exp(-g)) * u * share).astype(BF16)
        hidden_copy(b).start()

    for c in loads:
        c.wait()
    for c in swaps[:2]:
        c.wait_recv()
    for which, direction in streams:
        line_copy(which, direction, 1).start()
    for which, direction in streams:
        plane_copy(which, direction, 1, 0).start()
    swaps[2].wait_recv()

    line_arrives(1)
    plane_arrives(1, 0)
    for k in (2, 3):
        line_arrives(k)
        plane_arrives(1, 2 * k - 3)
        plane_arrives(1, 2 * k - 2)
    line_arrives(4)
    for rank in (5, 6, 7):
        plane_arrives(1, rank)
    for k in (2, 3):
        for rank in range(8):
            plane_arrives(k, rank)
            if rank == 2:
                compute(k - 2)
    for i in range(4):
        for rank in (HALF_RANKS[1][3 - i], HALF_RANKS[0][3 - i]):
            plane_arrives(4, rank)
        if i == 0:
            compute(2)
    compute(3)

    def own_terms(which, across):
        index = [cell(which, ORDER[7 - j], across) for j in range(8)]
        a = jnp.concatenate([hs[rows_of(i), :] for i in index], axis=0)
        b = jnp.concatenate([hr[rows_of(i), :] for i in index], axis=0)
        lanes = data_of[which]
        return jnp.dot(a, wd[pl.ds(0, quarter), lanes], preferred_element_type=F32) + jnp.dot(
            b, wd[pl.ds(quarter, quarter), lanes], preferred_element_type=F32
        )

    def big_index(direction, k, rank):
        if k == 4:
            return HALF_RANKS[direction].index(rank)
        return 4 + 8 * (3 - k) + 7 - rank

    def big_copy(which, direction, k, rank):
        st = 2 * which + direction
        i = 28 * st + big_index(direction, k, rank)
        return remote(
            s.at[rows_of(i), :], r.at[rows_of(i), :], b_send.at[st], b_recv.at[i], neighbour(which == 1, direction)
        )

    def big_sends(k, rank):
        ready = []
        for which, direction in streams:
            if k == 4 and rank not in HALF_RANKS[direction]:
                continue
            st = 2 * which + direction
            plane = 2 * which if k == 4 else st
            value = p[pl.ds((plane * 8 + 7 - rank) * chunk, chunk), :]
            if k < 3 or (k == 3 and rank in HALF_RANKS[direction]):
                before = big_copy(which, direction, k + 1, rank)
                before.wait_recv()
                i = 28 * st + big_index(direction, k + 1, rank)
                value += r[rows_of(i), :].astype(F32)
            i = 28 * st + big_index(direction, k, rank)
            s[rows_of(i), :] = value.astype(BF16)
            ready.append(big_copy(which, direction, k, rank))
        for c in ready:
            c.start()

    def line_sum(which, rank):
        value = p0[pl.ds((which * 8 + 7 - rank) * chunk, chunk), :]
        for direction in (FORWARD, BACKWARD):
            big_copy(which, direction, 1, rank).wait_recv()
            i = 28 * (2 * which + direction) + big_index(direction, 1, rank)
            value += r[rows_of(i), :].astype(F32)
        return value

    def small_copy(which, direction, k):
        i = 4 * (2 * which + direction) + 4 - k
        lanes = pl.ds(0, part)
        if k == 4:
            lanes = pl.ds(direction * (part // 2), part // 2)
        return remote(
            ss.at[rows_of(i), lanes], rs.at[rows_of(i), lanes], c_send.at[i], c_recv.at[i],
            neighbour(which == 0, direction),
        )

    def small_sends(k):
        ready = []
        for which in (0, 1):
            whole = line_sum(which, 7) if k == 4 else None
            for direction in (FORWARD, BACKWARD):
                i = 4 * (2 * which + direction) + 4 - k
                if k == 4:
                    lanes = slice(direction * (part // 2), (direction + 1) * (part // 2))
                    ss[rows_of(i), lanes] = whole[:, lanes].astype(BF16)
                else:
                    value = line_sum(which, ORDER.index(k if direction == FORWARD else -k))
                    small_copy(which, direction, k + 1).wait_recv()
                    if k == 3:
                        lo = value[:, : part // 2]
                        hi = value[:, part // 2 :]
                        came = rs[rows_of(i - 1), pl.ds(direction * (part // 2), part // 2)].astype(F32)
                        if direction == FORWARD:
                            lo = lo + came
                        else:
                            hi = hi + came
                        ss[rows_of(i), pl.ds(0, part // 2)] = lo.astype(BF16)
                        ss[rows_of(i), pl.ds(part // 2, part // 2)] = hi.astype(BF16)
                    else:
                        ss[rows_of(i), :] = (value + rs[rows_of(i - 1), :].astype(F32)).astype(BF16)
                ready.append(small_copy(which, direction, k))
        for c in ready:
            c.start()

    def fill(k):
        if k == 4:
            for which in (0, 1):
                p[pl.ds(2 * which * 8 * chunk, 8 * chunk), :] = own_terms(which, 4)
            return
        for which, direction in streams:
            st = 2 * which + direction
            p[pl.ds(st * 8 * chunk, 8 * chunk), :] = own_terms(which, k if direction == FORWARD else -k)

    weights[4].wait()
    swaps[3].wait_recv()
    for b in range(len(BLOCKS)):
        hidden_copy(b).wait_recv()
    fill(4)
    for i in range(4):
        big_sends(4, HALF_RANKS[0][i])
        big_sends(4, HALF_RANKS[1][i])
    for k in (3, 2):
        fill(k)
        for rank in range(7, -1, -1):
            big_sends(k, rank)
    fill(1)
    for which in (0, 1):
        p0[pl.ds(which * 8 * chunk, 8 * chunk), :] = own_terms(which, 0)
    for rank in (7, 6, 5):
        big_sends(1, rank)
    small_sends(4)
    for rank in (4, 3):
        big_sends(1, rank)
    small_sends(3)
    for rank in (2, 1):
        big_sends(1, rank)
    small_sends(2)
    big_sends(1, 0)
    small_sends(1)

    own = [None, None]
    for which in (0, 1):
        value = line_sum(which, 0)
        for direction in (FORWARD, BACKWARD):
            small_copy(which, direction, 1).wait_recv()
            value += rs[rows_of(4 * (2 * which + direction) + 3), :].astype(F32)
        upper, lower = value[:rows], value[rows:]
        own[which] = jnp.where(core == 0, upper, lower).astype(BF16)
        osend[:, data_of[which]] = jnp.where(core == 0, lower, upper).astype(BF16)
    swap = remote(osend, orecv, o_send, o_recv, sibling)
    swap.start()
    for which in (0, 1):
        start = pl.multiple_of(core * half + (part if which == 0 else 0), LANES)
        out[:, pl.ds(start, part)] = own[which]
    swap.wait_recv()
    out[:, pl.ds(theirs_from, half)] = orecv[...]

    swap.wait_send()
    for c in swaps:
        c.wait_send()
    for which, direction in streams:
        st = 2 * which + direction
        for k in (1, 2, 3, 4):
            line_copy(which, direction, k).wait_send()
            small_copy(which, direction, k).wait_send()
        span = x.at[rows_of(0, 28), lanes_of[which]]
        remote(span, span, g2_send.at[st], g2_recv.at[28 * st], neighbour(which == 1, direction)).wait_send()
        span = s.at[rows_of(28 * st, 28), :]
        remote(span, span, b_send.at[st], b_recv.at[28 * st], neighbour(which == 1, direction)).wait_send()
    for b in range(len(BLOCKS)):
        handed(b).wait_send()
        hidden_copy(b).wait_send()


def local(tokens, expert_ids, route_levels, gate_proj, up_proj, down_proj):
    rows, width = tokens.shape
    quarter = gate_proj.shape[2]
    half, chunk = width // 2, 2 * rows
    part = half // 2
    chips = lax.axis_size("expert")
    levels = jnp.sum(
        jnp.where(expert_ids[:, :, None] == jnp.arange(LANES, dtype=jnp.int32), route_levels[:, :, None], 0), axis=1
    ).astype(BF16)
    dma = pltpu.SemaphoreType.DMA
    any_space = pl.BlockSpec(memory_space=pl.ANY)
    return pl.pallas_call(
        kernel,
        out_shape=jax.ShapeDtypeStruct((rows, width), BF16),
        in_specs=[any_space] * 5,
        out_specs=pl.BlockSpec(memory_space=pltpu.VMEM),
        scratch_shapes=[
            pltpu.VMEM((chips * chunk, width + LANES), BF16),
            pltpu.VMEM((width, 2 * quarter), BF16),
            pltpu.VMEM((2 * quarter, half), BF16),
            pltpu.VMEM((chips * chunk, quarter), BF16),
            pltpu.VMEM((chips * chunk, quarter), BF16),
            pltpu.VMEM((4 * 8 * chunk, part), F32),
            pltpu.VMEM((2 * 8 * chunk, part), F32),
            pltpu.VMEM((4 * 28 * chunk, part), BF16),
            pltpu.VMEM((4 * 28 * chunk, part), BF16),
            pltpu.VMEM((16 * chunk, part), BF16),
            pltpu.VMEM((16 * chunk, part), BF16),
            pltpu.VMEM((rows, half), BF16),
            pltpu.VMEM((rows, half), BF16),
            dma((3,)), dma((5,)), dma((4,)), dma((4,)),
            dma((16,)), dma((16,)), dma((4,)), dma((112,)), dma((4,)), dma((4,)), dma((4,)), dma((4,)),
            dma((4,)), dma((112,)), dma((16,)), dma((16,)), dma(()), dma(()),
        ],
        compiler_params=pltpu.CompilerParams(
            collective_id=0, has_side_effects=True, vmem_limit_bytes=66 * 1024 * 1000
        ),
    )(tokens, levels, gate_proj, up_proj, down_proj)


def solution(mesh):
    return jax.shard_map(
        local,
        mesh=mesh,
        in_specs=(
            P(("replica", "expert", "sub"), None),
            P(("replica", "expert", "sub"), None),
            P(("replica", "expert", "sub"), None),
            P("expert", None, "sub"),
            P("expert", None, "sub"),
            P("expert", "sub", None),
        ),
        out_specs=P(("replica", "expert", "sub"), None),
        check_vma=False,
    )
```

time: 367 us -> 125 us (0.34)
  waiting for transfers between devices: 325 us -> 0 us
  Pallas kernels: 0 us -> 120 us
  matrix products: 25.2 us -> 0 us
  between operations: 13.5 us -> 0.02 us
    reduce_scatter x1 -> x0, waiting for transfers between devices: 213 us -> none  [local(): lax.psum_scatter(part, ('expert', 'sub'), scatter_dimension=0, tiled=True)]
    pallas_call x0 -> x1, Pallas kernels: none -> 120 us  [local(): pl.pallas_call(kernel, out_shape=jax.ShapeDtypeStruct((rows, width), BF16...]
    all_gather x1 -> x0, waiting for transfers between devices: 111 us -> none  [local(): everyone = lax.all_gather(carried, ('expert', 'sub'), axis=0, tiled=True)]
    dot_general x3 -> x0, matrix products: 25.2 us -> none  [the longest x1 9.36 us: local(): up = jnp.dot(x, up_proj[0], preferred_element_type=jnp.float32)]
  transfers between devices with their start and end apart: 2 -> 0, of which waited for: 2 -> 0; matrix products, arithmetic and copies ran while one was open for 0% -> 0% of each run, Pallas kernels for 0% -> 0%
where the time goes in v2:
time: 125 us; the launch traced here: 123 us
  Pallas kernels  120 us (96%)
  local copies, waits for them, and re-layouts  1.55 us (1%)
  other arithmetic  1.37 us (1%)
    pallas_call x1, Pallas kernels, local(): pl.pallas_call(kernel, out_shape=jax.ShapeDtypeStruct((rows, width), BF16...  120 us

profile of v2, /device:TPU:514, one launch (start us, length us, event | category | flops | bytes accessed | tf_op | source)
XLA Modules:
  0.0 122.7 jit_solution(14177058478760900199)
XLA Ops:
  0.0 0.8 select_reduce_fusion
  0.8 0.6 convert_element_type.3.levels
  1.4 119.8 %shard_map.64 = bf16[8,7168]{1,0:T(8,128)(2,1)} custom-call(bf16[8,7168]{1,0:T(8,128)(2,1)} %tokens.1, bf16[8,128]{1,0:T(8,128)(2,1)} %convert_element_type.3.levels, bf16[1,7168,256]{2,1,0:T(8,128)(2,1)} %gate.1, bf16[1,7168,256]{2,1,0:T(8,128)(2,1)} %up.1, bf16[1,256,7168]{2,1,0:T(8,128)(2,1)} %down.1), custom_call_target="tpu_custom_call" | custom-call | tf_op jit(solution)/shard_map/pallas_call | solution.py:405
  121.1 1.6 %copy.8 = bf16[8,7168]{1,0:T(8,128)(2,1)} copy(bf16[8,7168]{1,0:T(8,128)(2,1)} %shard_map.64) | data formatting | bytes 229376
